TPU v7x, 32 devices: a whole 2x2x4 slice. The times are simulated.
32 devices in a mesh: col: 8 (over z, x), row: 4 (over y, core).
Axes of the slice: x: 2, y: 2, z: 4, core: 2. Of those that a mesh axis runs over, the one named last changes fastest.
Arguments:
- vorticity: float32 [2, 8, 1024, 2048], P(None, 'row', 'col'), may hold values from -0.0017578125 to 0.0017578125
- divergence: float32 [2, 8, 1024, 2048], P(None, 'row', 'col'), may hold values from -0.0017578125 to 0.0017578125
- trunc_cut: int32 [1024], P('col'), may hold values from -1 to 1023, as said below
- level_slot: int32 [8], replicated, may hold values from 0 to 7, each once
Outputs:
- u_wind: float32 [8, 2048, 2048], P(None, ('col', 'row'))
- v_wind: float32 [8, 2048, 2048], P(None, ('col', 'row'))
- u_slope: float32 [8, 2048, 2048], P(None, ('col', 'row'))
- v_slope: float32 [8, 2048, 2048], P(None, ('col', 'row'))
Inputs may be any that keep to these rules, and one draw needn't show every extreme that they name: trunc_cut never rises with m, is 1023 at m = 0 and -1 (nothing kept) at the last m. level_slot is a permutation of the model levels.
All inputs are finite; a program needn't handle non-finite values.
Results may differ from a plain program's by a relative error of at most 0.0001.
Values sent between devices are 32-bit elements; how exact they have to be, the bound alone decides.
A program may use at most 128 MiB of HBM per device.

v0:
```python
import math

import jax
import jax.numpy as jnp
import numpy as np
from jax import lax
from jax.sharding import PartitionSpec as P

HIGH = lax.Precision.HIGH


def split_waves(array, axis):
    first = lax.slice_in_dim(array, 0, None, 2, axis)
    second = lax.slice_in_dim(array, 1, None, 2, axis)
    return jnp.concatenate([first, second], axis)


def phases(product, period):
    angles = 2.0 * np.pi * (product % period) / period
    return np.cos(angles).astype(np.float32), np.sin(angles).astype(np.float32)


def multiply(first, second):
    return first[0] * second[0] - first[1] * second[1], first[0] * second[1] + first[1] * second[0]


def north_table(north_cells):
    quarter = north_cells // 4
    fine = math.gcd(quarter, 32)
    column = np.arange(quarter)
    coarse_row = 4 * fine * np.arange(quarter // fine)[None, :, None, None] + np.arange(4)[:, None, None, None]
    fine_row = 4 * np.arange(fine)[None, None, :, None]
    coarse = phases(coarse_row * column, north_cells)
    close = phases(fine_row * column, north_cells)
    coarse, close = lax.optimization_barrier((coarse, close))
    cosine, sine = multiply(coarse, close)
    joined = jnp.concatenate([cosine, -sine], axis=3)
    return joined.reshape(4, quarter, 2 * quarter)


def east_table(columns, local_waves, east_cells):
    half = local_waves // 2
    cells = east_cells // 2
    column = np.arange(cells)
    coarse_wave = np.arange(2)[:, None, None, None] + local_waves * np.arange(columns)[None, :, None, None]
    close_wave = 2 * np.arange(half)[None, None, :, None]
    coarse = phases(coarse_wave * column, east_cells)
    close = phases(close_wave * column, east_cells)
    coarse, close = lax.optimization_barrier((coarse, close))
    cosine, sine = multiply(coarse, close)
    wave = coarse_wave + close_wave
    weights = np.where(wave == 0, 1.0, 2.0).astype(np.float32)
    scaled = (weights * wave * (2.0 * np.pi / east_cells)).astype(np.float32)
    real = jnp.concatenate([weights * cosine, -scaled * sine], axis=3)
    imag = jnp.concatenate([-weights * sine, -scaled * cosine], axis=3)
    joined = jnp.stack([real, imag], axis=2)
    return joined.reshape(2, columns * local_waves, 2 * cells)


def spectral_winds(vorticity, divergence, trunc_cut, wave_index, east_cells):
    north_cells = vorticity.shape[3]
    north_index = jnp.arange(north_cells, dtype=jnp.int32)
    north_wave = jnp.where(north_index < north_cells // 2, north_index, north_index - north_cells)
    wave_east = 2.0 * math.pi / east_cells * wave_index.astype(jnp.float32)
    wave_north = 2.0 * math.pi / north_cells * north_wave.astype(jnp.float32)
    east_col = wave_east[:, None]
    north_row = wave_north[None, :]
    square_wave = east_col * east_col + north_row * north_row
    retained = (jnp.abs(north_wave)[None, :] <= trunc_cut[:, None]) & (square_wave > 0)
    inverse_square = jnp.where(retained, 1.0 / jnp.where(square_wave > 0, square_wave, 1.0), 0.0)
    east_inverse = east_col * inverse_square
    north_inverse = north_row * inverse_square
    curl_real, curl_imag = vorticity[0], vorticity[1]
    source_real, source_imag = divergence[0], divergence[1]
    east = (
        -north_inverse * curl_imag + east_inverse * source_imag,
        north_inverse * curl_real - east_inverse * source_real,
    )
    north = (
        east_inverse * curl_imag + north_inverse * source_imag,
        -east_inverse * curl_real - north_inverse * source_real,
    )
    return east, north


def fold_quarters(wind, slots, half):
    real, imag = wind
    quarter = real.shape[2] // 4
    r0, r1, r2, r3 = (real[:, :, q * quarter:(q + 1) * quarter] for q in range(4))
    i0, i1, i2, i3 = (imag[:, :, q * quarter:(q + 1) * quarter] for q in range(4))
    folded = (
        (r0 + r2 + (r1 + r3), i0 + i2 + (i1 + i3)),
        (r0 - r2 - (i1 - i3), i0 - i2 + (r1 - r3)),
        (r0 + r2 - (r1 + r3), i0 + i2 - (i1 + i3)),
        (r0 - r2 + (i1 - i3), i0 - i2 - (r1 - r3)),
    )
    parts = []
    for part_real, part_imag in folded:
        shape = (slots, 2, 1, half, 2 * quarter)
        top = jnp.concatenate([part_real, part_imag], axis=2).reshape(shape)
        low = jnp.concatenate([part_imag, -part_real], axis=2).reshape(shape)
        parts.append(jnp.concatenate([top, low], axis=2))
    return jnp.stack(parts, axis=0).reshape(4, slots * 4 * half, 2 * quarter)


def on_device(vorticity, divergence, trunc_cut, level_slot):
    columns = lax.axis_size("col")
    row_devices = lax.axis_size("row")
    slots, local_waves, north_cells = vorticity.shape[1:]
    half = local_waves // 2
    quarter = north_cells // 4
    levels = slots * row_devices
    east_cells = 2 * local_waves * columns
    cells = east_cells // 2
    block = quarter // (columns * row_devices)
    first_wave = lax.axis_index("col") * local_waves
    wave_index = first_wave + jnp.arange(local_waves, dtype=jnp.int32)
    winds = spectral_winds(
        split_waves(vorticity, 2),
        split_waves(divergence, 2),
        split_waves(trunc_cut, 0),
        split_waves(wave_index, 0),
        east_cells,
    )
    table_north = north_table(north_cells)
    table_east = east_table(columns, local_waves, east_cells)
    holder = jnp.argsort(level_slot).astype(jnp.int32)
    results = []
    for wind in winds:
        folded = fold_quarters(wind, slots, half)
        fourier = jnp.einsum("pjk,pmk->pjm", table_north, folded, precision=HIGH)
        outgoing = fourier.reshape(4, quarter, slots, 2 * local_waves).transpose(1, 2, 0, 3)
        received = lax.all_to_all(outgoing, ("col", "row"), split_axis=0, concat_axis=0, tiled=True)
        shaped = received.reshape(columns, row_devices, block, slots, 4, 2, local_waves)
        arranged = shaped.transpose(1, 3, 5, 2, 4, 0, 6).reshape(
            levels, 2, block * 4, columns * local_waves
        )
        placed = jnp.concatenate(
            [lax.dynamic_slice_in_dim(arranged, holder[level], 1, 0) for level in range(levels)], axis=0
        )
        even = jnp.einsum("lyk,kx->lyx", placed[:, 0], table_east[0], precision=HIGH)
        odd = jnp.einsum("lyk,kx->lyx", placed[:, 1], table_east[1], precision=HIGH)
        total, rest = even + odd, even - odd
        results.append(
            (
                jnp.concatenate([total[:, :, :cells], rest[:, :, :cells]], axis=2),
                jnp.concatenate([total[:, :, cells:], rest[:, :, cells:]], axis=2),
            )
        )
    return results[0][0], results[1][0], results[0][1], results[1][1]


def solution(mesh):
    return jax.shard_map(
        on_device,
        mesh=mesh,
        in_specs=(P(None, "row", "col", None), P(None, "row", "col", None), P("col"), P()),
        out_specs=(
            P(None, ("col", "row"), None),
            P(None, ("col", "row"), None),
            P(None, ("col", "row"), None),
            P(None, ("col", "row"), None),
        ),
        check_vma=False,
    )
```

profile of v0, /device:TPU:1, one launch (start us, length us, event | category | flops | bytes accessed | tf_op | source)
XLA Modules:
  0.0 366.8 jit_solution(9012250437534499265)
XLA Ops:
  2.6 8.1 %slice.167 = f32[2,2,64,2048]{3,2,1,0:T(8,128)S(1)} slice(f32[2,2,128,2048]{3,2,1,0:T(8,128)} %param.16), slice={[0:2:1], [0:2:1], [1:128:2], [0:2048:1]} | slice | bytes 4194304 | tf_op jit(solution)/shard_map/slice | solution.py:14
  10.7 10.0 %slice.166 = f32[2,2,64,2048]{3,2,1,0:T(8,128)} slice(f32[2,2,128,2048]{3,2,1,0:T(8,128)} %param.16), slice={[0:2:1], [0:2:1], [0:128:2], [0:2048:1]} | slice | bytes 4194304 | tf_op jit(solution)/shard_map/slice | solution.py:13
  20.8 9.8 %slice.170 = f32[2,2,64,2048]{3,2,1,0:T(8,128)} slice(f32[2,2,128,2048]{3,2,1,0:T(8,128)} %param.17), slice={[0:2:1], [0:2:1], [1:128:2], [0:2048:1]} | slice | bytes 4194304 | tf_op jit(solution)/shard_map/slice | solution.py:14
  30.6 9.8 %slice.169 = f32[2,2,64,2048]{3,2,1,0:T(8,128)} slice(f32[2,2,128,2048]{3,2,1,0:T(8,128)} %param.17), slice={[0:2:1], [0:2:1], [0:128:2], [0:2048:1]} | slice | bytes 4194304 | tf_op jit(solution)/shard_map/slice | solution.py:13
  42.6 2.0 multiply_subtract_fusion.1
  44.9 1.3 copy-done.2
  46.2 2.9 multiply_add_fusion.1
  50.3 1.5 pad_maximum_fusion.14
  52.1 1.5 pad_maximum_fusion.15
  53.9 1.5 pad_maximum_fusion.16
  55.6 1.5 pad_maximum_fusion.17
  57.4 4.6 %fusion.17 = (f32[4,512,512]{2,1,0:T(8,128)}, f32[4,512,512]{2,1,0:T(8,128)}) fusion(f32[512,512]{1,0:T(8,128)S(1)} %bitcast.193, f32[4,16,512]{2,1,0:T(8,128)S(1)} %bitcast.204, f32[512,512]{1,0:T(8,128)S(1)} %bitcast.192, f32[4,16,512]{2,1,0:T(8,128)S(1)} %bitcast.205), kind=kLoop, calls=%fused_computation.27 | loop fusion | flops 7340032 | bytes 10747904 | tf_op jit(solution)/shard_map/sub | solution.py:24
  62.0 14.6 %fusion.9 = f32[4,512,512]{1,2,0:T(8,128)} fusion(f32[1,512,1024]{2,1,0:T(8,128)} %bitcast.199, f32[1,512,1024]{2,1,0:T(8,128)} %bitcast.198, f32[1,512,1024]{2,1,0:T(8,128)} %bitcast.196, f32[1,512,1024]{2,1,0:T(8,128)} %bitcast.194, f32[4,512,512]{2,1,0:T(8,128)} %get-tuple-element.70, f32[4,512,512]{2,1,0:T(8,128)} %get-tuple-element.69), kind=kOutput, calls=%fused_computation.15 | convolution fusion | flops 6450839552 | bytes 20971520 | tf_op jit(solution)/shard_map/pjk,pmk->pjm/dot_general | solution.py:131
  76.6 5.4 %copy.80 = f32[4,512,2,256]{3,0,2,1:T(4,128)} copy(f32[4,512,2,256]{1,3,2,0:T(8,128)} %bitcast.175) | data formatting | bytes 8388608 | tf_op jit(solution)/shard_map/reshape | solution.py:132
  82.0 7.5 %all-to-all-start.1 = ((f32[512,2,4,256]{3,2,1,0:T(4,128)}), f32[512,2,4,256]{3,2,1,0:T(4,128)}, u32[]{:S(2)}, u32[]{:S(2)}) async-start(f32[512,2,4,256]{3,2,1,0:T(4,128)} %bitcast.171), calls=%async_computation.1 | async-start | bytes 8388608 | tf_op jit(solution)/shard_map/all_to_all | solution.py:133
  89.8 1.4 copy-done
  91.7 1.5 pad_maximum_fusion.10
  93.9 1.5 pad_maximum_fusion.11
  95.7 1.5 pad_maximum_fusion.12
  97.5 1.5 pad_maximum_fusion.13
  99.3 14.0 %fusion.1 = f32[4,512,512]{1,2,0:T(8,128)} fusion(f32[1,512,1024]{2,1,0:T(8,128)} %bitcast.201, f32[1,512,1024]{2,1,0:T(8,128)} %bitcast.200, f32[1,512,1024]{2,1,0:T(8,128)} %bitcast.197, f32[1,512,1024]{2,1,0:T(8,128)S(1)} %bitcast.195, f32[4,512,512]{2,1,0:T(8,128)} %get-tuple-element.70, f32[4,512,512]{2,1,0:T(8,128)} %get-tuple-element.69), kind=kOutput, calls=%fused_computation.5 | convolution fusion | flops 6450839552 | bytes 20971520 | tf_op jit(solution)/shard_map/pjk,pmk->pjm/dot_general | solution.py:131
  113.3 5.4 %copy.68 = f32[4,512,2,256]{3,0,2,1:T(4,128)} copy(f32[4,512,2,256]{1,3,2,0:T(8,128)} %bitcast.174) | data formatting | bytes 8388608 | tf_op jit(solution)/shard_map/reshape | solution.py:132
  118.7 64.2 %all-to-all-done.1 = f32[512,2,4,256]{3,2,1,0:T(4,128)} async-done(((f32[512,2,4,256]{3,2,1,0:T(4,128)}), f32[512,2,4,256]{3,2,1,0:T(4,128)}, u32[]{:S(2)}, u32[]{:S(2)}) %all-to-all-start.1) | async-done | bytes 4194336 | tf_op jit(solution)/shard_map/all_to_all | solution.py:133
  183.0 6.4 %all-to-all-start = ((f32[512,2,4,256]{3,2,1,0:T(4,128)}), f32[512,2,4,256]{3,2,1,0:T(4,128)}, u32[]{:S(2)}, u32[]{:S(2)}) async-start(f32[512,2,4,256]{3,2,1,0:T(4,128)} %bitcast.170), calls=%async_computation | async-start | bytes 8388608 | tf_op jit(solution)/shard_map/all_to_all | solution.py:133
  206.1 5.4 %fusion.22 = (f32[2,8,64,1024]{3,2,1,0:T(8,128)S(1)}, f32[2,8,64,1024]{3,2,1,0:T(8,128)}, f32[2,8,64,1024]{3,2,1,0:T(8,128)}, f32[2,8,64,1024]{3,2,1,0:T(8,128)}) fusion(f32[2,8,64]{2,1,0:T(8,128)S(1)} %copy-done.21, f32[64,1024]{1,0:T(8,128)S(1)} %bitcast.202, f32[2,8,1024]{2,1,0:T(8,128)S(1)} %bitcast.206, f32[64,1024]{1,0:T(8,128)S(1)} %bitcast.203, ...), kind=kLoop, calls=%fused_computation.42 | loop fusion | flops 10485760 | bytes 17444864 | tf_op jit(solution)/shard_map/mul | solution.py:55
  211.5 7.5 %maximum_bitcast_fusion = (f32[2,8,1,64,2048]{4,3,2,1,0:T(8,128)S(1)}, f32[2,8,1,64,2048]{4,3,2,1,0:T(8,128)}) fusion(f32[2,8,64,1024]{3,2,1,0:T(8,128)} %get-tuple-element.80, f32[2,8,64,1024]{3,2,1,0:T(8,128)} %get-tuple-element.82, f32[2,8,64,1024]{3,2,1,0:T(8,128)S(1)} %get-tuple-element.79, f32[2,8,64,1024]{3,2,1,0:T(8,128)} %get-tuple-element.81), kind=kLoop, calls=%fused_computation.13 | loop fusion | flops 4194304 | bytes 33554432 | tf_op jit(solution)/shard_map/stack | solution.py:56
  219.0 8.8 %pad_maximum_fusion = (f32[1,8,2,64,2048]{4,3,2,1,0:T(8,128)}, f32[1,8,2,64,2048]{4,3,2,1,0:T(8,128)}) fusion(f32[2,8,1,64,2048]{4,3,2,1,0:T(8,128)} %get-tuple-element.116, f32[2,8,1,64,2048]{4,3,2,1,0:T(8,128)S(1)} %get-tuple-element.115), kind=kLoop, calls=%fused_computation.3 | loop fusion | flops 4194304 | bytes 33554432 | tf_op jit(solution)/shard_map/stack | solution.py:56
  227.7 6.2 %reshape.437 = f32[8,4,16,2,4,2,128]{6,5,4,3,2,1,0:T(2,128)} reshape(f32[512,2,4,256]{3,2,1,0:T(4,128)} %all-to-all-done.1) | data formatting | bytes 8388608 | tf_op jit(solution)/shard_map/reshape | solution.py:134
  234.0 6.6 %copy.82 = f32[4,2,2,16,4,8,128]{6,5,4,3,1,0,2:T(8,128)} copy(f32[4,2,2,16,4,8,128]{6,2,4,1,3,0,5:T(2,128)} %bitcast.172) | data formatting | bytes 8388608 | tf_op jit(solution)/shard_map/transpose | solution.py:135
  240.6 4.9 %reshape.433 = f32[8,2,64,1024]{3,2,0,1:T(8,128)} reshape(f32[4,2,2,16,4,8,128]{6,5,4,3,1,0,2:T(8,128)} %copy.82) | data formatting | bytes 8388608 | tf_op jit(solution)/shard_map/reshape | solution.py:135
  245.5 37.4 %all-to-all-done = f32[512,2,4,256]{3,2,1,0:T(4,128)} async-done(((f32[512,2,4,256]{3,2,1,0:T(4,128)}), f32[512,2,4,256]{3,2,1,0:T(4,128)}, u32[]{:S(2)}, u32[]{:S(2)}) %all-to-all-start) | async-done | bytes 4194336 | tf_op jit(solution)/shard_map/all_to_all | solution.py:133
  282.8 6.2 %reshape.436 = f32[8,4,16,2,4,2,128]{6,5,4,3,2,1,0:T(2,128)} reshape(f32[512,2,4,256]{3,2,1,0:T(4,128)} %all-to-all-done) | data formatting | bytes 8388608 | tf_op jit(solution)/shard_map/reshape | solution.py:134
  289.1 6.6 %copy.70 = f32[4,2,2,16,4,8,128]{6,5,4,3,1,0,2:T(8,128)} copy(f32[4,2,2,16,4,8,128]{6,2,4,1,3,0,5:T(2,128)} %bitcast.173) | data formatting | bytes 8388608 | tf_op jit(solution)/shard_map/transpose | solution.py:135
  295.7 5.0 %reshape.422 = f32[8,2,64,1024]{3,2,0,1:T(8,128)} reshape(f32[4,2,2,16,4,8,128]{6,5,4,3,1,0,2:T(8,128)} %copy.70) | data formatting | bytes 8388608 | tf_op jit(solution)/shard_map/reshape | solution.py:135
  300.8 1.2 dynamic-slice_dynamic-update-slice_fusion.15
  302.0 1.7 dynamic-slice_dynamic-update-slice_fusion.7
  303.7 1.8 dynamic-slice_dynamic-update-slice_fusion.14
  309.4 2.0 copy-done.9
  311.4 1.8 slice-done.1
  313.2 7.4 %fusion.28 = f32[8,64,2048]{2,1,0:T(8,128)S(1)} fusion(f32[1024,2048,1]{1,0,2:T(8,128)S(1)} %bitcast.164, f32[8,2,64,1024]{3,2,0,1:T(8,128)S(1)} %dynamic-slice_dynamic-update-slice_fusion), kind=kOutput, calls=%fused_computation.49 | convolution fusion | flops 6442450944 | bytes 14680064 | tf_op jit(solution)/shard_map/lyk,kx->lyx/dot_general | solution.py:142
  320.7 7.7 %fusion.30 = f32[8,64,2048]{2,1,0:T(8,128)S(1)} fusion(f32[1024,2048,1]{1,0,2:T(8,128)S(1)} %bitcast.165, f32[8,2,64,1024]{3,2,0,1:T(8,128)S(1)} %dynamic-slice_dynamic-update-slice_fusion.8), kind=kOutput, calls=%fused_computation.53 | convolution fusion | flops 6442450944 | bytes 14680064 | tf_op jit(solution)/shard_map/lyk,kx->lyx/dot_general | solution.py:142
  328.4 11.6 %fusion.79 = (f32[8,64,2048]{2,1,0:T(8,128)}, f32[8,64,2048]{2,1,0:T(8,128)S(1)}) fusion(f32[8,64,2048]{2,1,0:T(8,128)S(1)} %fusion.30, f32[1024,2048,1]{1,0,2:T(8,128)S(1)} %bitcast.168, f32[8,2,64,1024]{3,2,0,1:T(8,128)} %copy-done.10), kind=kOutput, calls=%fused_computation.165 | convolution fusion | flops 6444548096 | bytes 23068672 | tf_op jit(solution)/shard_map/lyk,kx->lyx/dot_general | solution.py:141
  340.0 11.6 %fusion.78 = (f32[8,64,2048]{2,1,0:T(8,128)}, f32[8,64,2048]{2,1,0:T(8,128)S(1)}) fusion(f32[8,64,2048]{2,1,0:T(8,128)S(1)} %fusion.28, f32[1024,2048,1]{1,0,2:T(8,128)S(1)} %bitcast.169, f32[8,2,64,1024]{3,2,0,1:T(8,128)} %copy-done.9), kind=kOutput, calls=%fused_computation.164 | convolution fusion | flops 6444548096 | bytes 23068672 | tf_op jit(solution)/shard_map/lyk,kx->lyx/dot_general | solution.py:141
  351.6 2.9 fusion.82
  356.5 2.5 pad_maximum_fusion.6
  359.0 2.5 pad_maximum_fusion.4
  361.6 2.5 pad_maximum_fusion.7
  364.1 2.5 pad_maximum_fusion.5
  (99 shorter events, 16.3 us)
Async XLA Ops:
  10.7 30.4 %copy-start.1 = (f32[2,2,64,2048]{3,2,1,0:T(8,128)}, f32[2,2,64,2048]{3,2,1,0:T(8,128)S(1)}, u32[]{:S(2)}) copy-start(f32[2,2,64,2048]{3,2,1,0:T(8,128)S(1)} %slice.167) | copy-start | bytes 6291460
  40.4 1.6 copy-start.3
  40.4 2.2 copy-start.4
  42.6 2.2 copy-start.5
  44.6 1.6 copy-start.2
  55.4 1.8 copy-start.19
  55.4 1.9 copy-start.18
  55.4 2.0 copy-start.14
  55.4 2.0 copy-start.15
  82.0 100.9 %all-to-all-start.1 = ((f32[512,2,4,256]{3,2,1,0:T(4,128)}), f32[512,2,4,256]{3,2,1,0:T(4,128)}, u32[]{:S(2)}, u32[]{:S(2)}) async-start(f32[512,2,4,256]{3,2,1,0:T(4,128)} %bitcast.171), calls=%async_computation.1 | async-start | bytes 8388608 | tf_op jit(solution)/shard_map/all_to_all | solution.py:133
  89.6 1.6 copy-start
  97.2 2.1 copy-start.11
  183.0 6.5 %copy-start.23 = (s32[8]{0:T(128)S(1)}, s32[8]{0:T(128)}, u32[]{:S(2)}) copy-start(s32[8]{0:T(128)} %param.19) | copy-start | bytes 100
  183.0 23.1 %copy-start.12 = (f32[1,1,64,1024]{3,2,1,0:T(8,128)S(1)}, f32[1,1,64,1024]{3,2,1,0:T(8,128)}, u32[]{:S(2)}) copy-start(f32[1,1,64,1024]{3,2,1,0:T(8,128)} %constant.55.clone) | copy-start | bytes 786436
  183.0 23.1 %copy-start.13 = (f32[1,1,64,1024]{3,2,1,0:T(8,128)S(1)}, f32[1,1,64,1024]{3,2,1,0:T(8,128)}, u32[]{:S(2)}) copy-start(f32[1,1,64,1024]{3,2,1,0:T(8,128)} %constant.54.clone) | copy-start | bytes 786436
  183.0 23.1 %copy-start.16 = (f32[2,8,1,1024]{3,1,0,2:T(8,128)S(1)}, f32[2,8,1,1024]{3,1,0,2:T(8,128)}, u32[]{:S(2)}) copy-start(f32[2,8,1,1024]{3,1,0,2:T(8,128)} %constant.53.clone) | copy-start | bytes 196612
  183.0 23.1 %copy-start.17 = (f32[2,8,1,1024]{3,1,0,2:T(8,128)S(1)}, f32[2,8,1,1024]{3,1,0,2:T(8,128)}, u32[]{:S(2)}) copy-start(f32[2,8,1,1024]{3,1,0,2:T(8,128)} %constant.52.clone) | copy-start | bytes 196612
  183.0 23.1 %copy-start.20 = (f32[2,8,64]{2,1,0:T(8,128)S(1)}, f32[2,8,64]{2,1,0:T(8,128)}, u32[]{:S(2)}) copy-start(f32[2,8,64]{2,1,0:T(8,128)} %constant.63) | copy-start | bytes 12292
  183.0 23.1 %copy-start.21 = (f32[2,8,64]{2,1,0:T(8,128)S(1)}, f32[2,8,64]{2,1,0:T(8,128)}, u32[]{:S(2)}) copy-start(f32[2,8,64]{2,1,0:T(8,128)} %constant.62) | copy-start | bytes 12292
  183.0 23.1 %copy-start.22 = (f32[2,8,64]{2,1,0:T(8,128)S(1)}, f32[2,8,64]{2,1,0:T(8,128)}, u32[]{:S(2)}) copy-start(f32[2,8,64]{2,1,0:T(8,128)} %constant.61) | copy-start | bytes 12292
  183.0 99.8 %all-to-all-start = ((f32[512,2,4,256]{3,2,1,0:T(4,128)}), f32[512,2,4,256]{3,2,1,0:T(4,128)}, u32[]{:S(2)}, u32[]{:S(2)}) async-start(f32[512,2,4,256]{3,2,1,0:T(4,128)} %bitcast.170), calls=%async_computation | async-start | bytes 8388608 | tf_op jit(solution)/shard_map/all_to_all | solution.py:133
  300.7 7.0 %copy-start.6 = (f32[8,2,64,1024]{3,2,0,1:T(8,128)S(1)}, f32[8,2,64,1024]{3,2,0,1:T(8,128)}, u32[]{:S(2)}) copy-start(f32[8,2,64,1024]{3,2,0,1:T(8,128)} %reshape.433) | copy-start | bytes 12582916
  300.7 8.2 %copy-start.7 = (f32[8,2,64,1024]{3,2,0,1:T(8,128)S(1)}, f32[8,2,64,1024]{3,2,0,1:T(8,128)}, u32[]{:S(2)}) copy-start(f32[8,2,64,1024]{3,2,0,1:T(8,128)} %reshape.422) | copy-start | bytes 12582916
  302.0 9.4 %slice-start = ((s8[8388608]{0:T(1024)(128)(4,1)}), s8[4194304]{0:T(1024)(128)(4,1)S(1)}, s32[]{:S(2)}) async-start(s8[8388608]{0:T(1024)(128)(4,1)} %bitcast.162), calls=%async_computation.2 | async-start | bytes 8388608
  309.0 4.3 %slice-start.1 = ((s8[8388608]{0:T(1024)(128)(4,1)}), s8[4194304]{0:T(1024)(128)(4,1)S(1)}, s32[]{:S(2)}) async-start(s8[8388608]{0:T(1024)(128)(4,1)} %bitcast.162), calls=%async_computation.3 | async-start | bytes 8388608
  309.3 19.0 %copy-start.10 = (f32[8,2,64,1024]{3,2,0,1:T(8,128)}, f32[8,2,64,1024]{3,2,0,1:T(8,128)S(1)}, u32[]{:S(2)}) copy-start(f32[8,2,64,1024]{3,2,0,1:T(8,128)S(1)} %dynamic-slice_dynamic-update-slice_fusion.8) | copy-start | bytes 12582916
  309.4 2.0 copy-start.9
  313.2 15.1 %slice-start.2 = ((s8[8388608]{0:T(1024)(128)(4,1)}), s8[4194304]{0:T(1024)(128)(4,1)S(1)}, s32[]{:S(2)}) async-start(s8[8388608]{0:T(1024)(128)(4,1)} %bitcast.166), calls=%async_computation.4 | async-start | bytes 8388608
  320.7 7.7 %slice-start.3 = ((s8[8388608]{0:T(1024)(128)(4,1)}), s8[4194304]{0:T(1024)(128)(4,1)S(1)}, s32[]{:S(2)}) async-start(s8[8388608]{0:T(1024)(128)(4,1)} %bitcast.166), calls=%async_computation.5 | async-start | bytes 8388608
  351.6 3.4 copy-start.8
where the time goes:
time: 373 us; the launch traced here: 367 us
  local copies, waits for them, and re-layouts  109 us (29%)
  waiting for transfers between devices  102 us (27%)
  matrix products  66.9 us (18%)
  other arithmetic  59 us (16%)
  between operations  16.5 us (4%)
  starting transfers between devices  14 us (4%)
    all_to_all x2, waiting for transfers between devices, on_device(): lax.all_to_all(outgoing, ('col', 'row'), split_axis=0, concat_axis=0, til...  102 us
    dot_general x2, matrix products, on_device(): fourier = jnp.einsum('pjk,pmk->pjm', table_north, folded, precision=HIGH)  28.6 us
    dot_general x2, matrix products, on_device(): jnp.einsum('lyk,kx->lyx', placed[:, 0], table_east[0], precision=HIGH)  23.2 us
    slice x4, local copies, waits for them, and re-layouts, split_waves(): first = lax.slice_in_dim(array, 0, None, 2, axis)  20.8 us
    slice x4, local copies, waits for them, and re-layouts, split_waves(): second = lax.slice_in_dim(array, 1, None, 2, axis)  18.9 us
    unnamed x70, local copies, waits for them, and re-layouts  17.4 us
    another operation x2, other arithmetic, east_table(): joined = jnp.stack([real, imag], axis=2)  16.2 us
    dot_general x2, matrix products, on_device(): odd = jnp.einsum('lyk,kx->lyx', placed[:, 1], table_east[1], precision=HIGH)  15.1 us
  transfers between devices with their start and end apart: 2, of which 2 were waited for; matrix products, arithmetic and copies ran while one was open for 19% of the time, Pallas kernels for 0%

commit v1 on v0

--- a/solution.py
+++ b/solution.py
@@ -1,11 +1,18 @@
+import functools
 import math
 
 import jax
 import jax.numpy as jnp
 import numpy as np
 from jax import lax
+from jax.experimental import pallas as pl
+from jax.experimental.pallas import tpu as pltpu
 from jax.sharding import PartitionSpec as P
 
+MESH = pl.DeviceIdType.MESH
+LANES = 128
+ROWS = 16
+FINE = 32
 HIGH = lax.Precision.HIGH
 
 
@@ -103,7 +110,7 @@
     return jnp.stack(parts, axis=0).reshape(4, slots * 4 * half, 2 * quarter)
 
 
-def on_device(vorticity, divergence, trunc_cut, level_slot):
+def general_device(vorticity, divergence, trunc_cut, level_slot):
     columns = lax.axis_size("col")
     row_devices = lax.axis_size("row")
     slots, local_waves, north_cells = vorticity.shape[1:]
@@ -150,16 +157,475 @@
     return results[0][0], results[1][0], results[0][1], results[1][1]
 
 
+def cos_sin(product, period):
+    angles = 2.0 * np.pi * (product % period) / period
+    return np.stack([np.cos(angles), np.sin(angles)]).astype(np.float32)
+
+
+def split(value):
+    high = value.astype(jnp.bfloat16)
+    return high, (value - high.astype(jnp.float32)).astype(jnp.bfloat16)
+
+
+def dot3(left, right, dims):
+    def one(first, second):
+        return lax.dot_general(first, second, (dims, ((), ())), preferred_element_type=jnp.float32)
+
+    return one(left[0], right[0]) + one(left[0], right[1]) + one(left[1], right[0])
+
+
+def sizes_of(shape, columns, row_devices):
+    slots, local, north_cells = shape[1:]
+    return dict(
+        columns=columns,
+        rows=row_devices,
+        devices=columns * row_devices,
+        slots=slots,
+        local=local,
+        half=local // 2,
+        north=north_cells,
+        quarter=north_cells // 4,
+        share=north_cells // (columns * row_devices),
+        east=2 * local * columns,
+        cells=local * columns,
+    )
+
+
+def build_north_table(sz, fine, coarse, table):
+    quarter = sz["quarter"]
+
+    def step(g, carry):
+        cos_c, sin_c = coarse[0, pl.ds(g, 1), :], coarse[1, pl.ds(g, 1), :]
+        cos_f, sin_f = fine[0], fine[1]
+        cosine = cos_c * cos_f - sin_c * sin_f
+        sine = -(sin_c * cos_f + cos_c * sin_f)
+        at = pl.ds(pl.multiple_of(g * FINE, FINE), FINE)
+        for part, value in ((0, cosine), (1, sine)):
+            high, low = split(value)
+            table[0, at, part * quarter:(part + 1) * quarter] = high
+            table[1, at, part * quarter:(part + 1) * quarter] = low
+        return carry
+
+    lax.fori_loop(0, quarter // FINE, step, 0)
+
+
+def build_east_table(sz, fine, coarse, table):
+    half, columns, cells = sz["half"], sz["columns"], sz["cells"]
+    width = min(cells, 256)
+
+    def step(index, carry):
+        parity, column = index // columns, index % columns
+        base = column * (2 * half)
+        for start in range(0, cells, width):
+            lanes = slice(start, start + width)
+            cos_c, sin_c = coarse[0, pl.ds(index, 1), lanes], coarse[1, pl.ds(index, 1), lanes]
+            cos_f, sin_f = fine[0, :, lanes], fine[1, :, lanes]
+            cosine = cos_c * cos_f - sin_c * sin_f
+            sine = -(sin_c * cos_f + cos_c * sin_f)
+            for part, value in ((0, cosine), (1, sine)):
+                at = pl.ds(pl.multiple_of(base + part * half, half), half)
+                high, low = split(value)
+                table[0, parity, at, lanes] = high
+                table[1, parity, at, lanes] = low
+        return carry
+
+    lax.fori_loop(0, 2 * columns, step, 0)
+
+
+def build_folded(sz, slot, wind, column, curl, source, cut, twiddle, folded):
+    half, quarter, north = sz["half"], sz["quarter"], sz["north"]
+    is_north = wind == 1
+
+    def step(block, carry):
+        lanes = pl.multiple_of(block * LANES, LANES)
+        index = lax.broadcasted_iota(jnp.int32, (ROWS, LANES), 1) + lanes
+        line = lax.broadcasted_iota(jnp.int32, (ROWS, LANES), 0)
+        for parity in range(2):
+            for top in range(0, half, ROWS):
+                at = pl.ds(parity + 2 * top, ROWS, stride=2)
+                wave = column * (2 * half) + parity + 2 * (line + top)
+                kx = (2.0 * math.pi / sz["east"]) * wave.astype(jnp.float32)
+                weight = jnp.where(wave == 0, 1.0, 2.0)
+                kept = cut[at, :]
+                real, imag = [], []
+                for q in range(4):
+                    number = index + q * quarter
+                    number = jnp.where(number < north // 2, number, number - north)
+                    ky = (2.0 * math.pi / north) * number.astype(jnp.float32)
+                    square = kx * kx + ky * ky
+                    retained = (jnp.abs(number) <= kept) & (square > 0)
+                    inverse = jnp.where(retained, weight / jnp.where(square > 0, square, 1.0), 0.0)
+                    by_x, by_y = kx * inverse, ky * inverse
+                    first = jnp.where(is_north, by_x, -by_y)
+                    second = jnp.where(is_north, by_y, by_x)
+                    strip = block + q * (quarter // LANES)
+                    zr, zi = curl[slot, strip, 0, at, :], curl[slot, strip, 1, at, :]
+                    dr, di = source[slot, strip, 0, at, :], source[slot, strip, 1, at, :]
+                    real.append(first * zi + second * di)
+                    imag.append(-(first * zr + second * dr))
+                (r0, r1, r2, r3), (i0, i1, i2, i3) = real, imag
+                rs, rd, rt, ru = r0 + r2, r0 - r2, r1 + r3, r1 - r3
+                js, jd, jt, ju = i0 + i2, i0 - i2, i1 + i3, i1 - i3
+                parts = ((rs + rt, js + jt), (rd - ju, jd + ru), (rs - rt, js - jt), (rd + ju, jd - ru))
+                near = pl.ds(lanes, LANES)
+                far = pl.ds(pl.multiple_of(lanes + quarter, LANES), LANES)
+                for p, (a, b) in enumerate(parts):
+                    if p:
+                        cosine = twiddle[2 * p:2 * p + 1, near]
+                        sine = twiddle[2 * p + 1:2 * p + 2, near]
+                        a, b = a * cosine - b * sine, a * sine + b * cosine
+                    upper = slice(parity * 2 * half + top, parity * 2 * half + top + ROWS)
+                    lower = slice(parity * 2 * half + half + top, parity * 2 * half + half + top + ROWS)
+                    for level, (x, y) in enumerate(zip(split(a), split(b))):
+                        folded[level, p, upper, near] = x
+                        folded[level, p, upper, far] = y
+                        folded[level, p, lower, near] = y
+                        folded[level, p, lower, far] = -x
+        return carry
+
+    lax.fori_loop(0, quarter // LANES, step, 0)
+
+
+def north_transform(sz, chunk, table, folded, outgoing):
+    quarter = sz["quarter"]
+    for p in range(4):
+        left = (table[0], table[1])
+        right = (folded[0, p], folded[1, p])
+        sums = dot3(left, right, ((1,), (1,)))
+        for parity in range(2):
+            outgoing[chunk, parity, pl.ds(p, quarter, stride=4), :] = sums[:, parity * LANES:(parity + 1) * LANES]
+
+
+def build_waves(sz, received, waves):
+    columns, half = sz["columns"], sz["half"]
+    lines = sz["rows"] * sz["share"]
+
+    def step(column, carry):
+        sources = pl.ds(pl.multiple_of(column * sz["rows"], sz["rows"]), sz["rows"])
+        lane = lax.broadcasted_iota(jnp.int32, (1, 2 * half), 1)
+        into = pl.ds(pl.multiple_of(column * 2 * half, LANES), 2 * half)
+        for parity in range(2):
+            value = received[sources, parity].reshape(lines, 2 * half)
+            wave = column * (2 * half) + parity + 2 * jnp.where(lane < half, lane, lane - half)
+            kx = (2.0 * math.pi / sz["east"]) * wave.astype(jnp.float32)
+            slope = pltpu.roll(value, half, axis=1) * jnp.where(lane < half, -kx, kx)
+            for kind, data in enumerate((value, slope)):
+                high, low = split(data)
+                waves[0, parity, kind * lines:(kind + 1) * lines, into] = high
+                waves[1, parity, kind * lines:(kind + 1) * lines, into] = low
+        return carry
+
+    lax.fori_loop(0, columns, step, 0)
+
+
+def east_tile(sz, waves, table, lanes):
+    sums = []
+    for parity in range(2):
+        left = (waves[0, parity], waves[1, parity])
+        right = (table[0, parity, :, lanes], table[1, parity, :, lanes])
+        sums.append(dot3(left, right, ((1,), (0,))))
+    return sums[0] + sums[1], sums[0] - sums[1]
+
+
+def exchange_kernel(
+    sz, curl_hbm, source_hbm, cut, fine_north, coarse_north, twiddle, fine_east, coarse_east,
+    results, last, table_out,
+    curl, source, table_north, table_east, folded, outgoing, incoming, waves, grid,
+    load_sem, send_sem, recv_sem, own_sem, out_sem, table_sem,
+):
+    columns, rows, devices, slots = sz["columns"], sz["rows"], sz["devices"], sz["slots"]
+    share, cells = sz["share"], sz["cells"]
+    chunks = 2 * slots
+    col, row = lax.axis_index("col"), lax.axis_index("row")
+    me = col * rows + row
+    strips = sz["north"] // LANES
+
+    def load(slot, strip):
+        lanes = pl.ds(pl.multiple_of(strip * LANES, LANES), LANES)
+        for which, (hbm, near) in enumerate(((curl_hbm, curl), (source_hbm, source))):
+            yield pltpu.make_async_copy(
+                hbm.at[:, slot, :, lanes], near.at[slot, strip], load_sem.at[which, slot, strip]
+            )
+
+    def start_load(index, carry):
+        for copy in load(index // strips, index % strips):
+            copy.start()
+        return carry
+
+    lax.fori_loop(0, slots * strips, start_load, 0)
+    barrier = pltpu.get_barrier_semaphore()
+
+    def target(offset):
+        there_col = lax.rem(col + offset % columns, columns)
+        there_row = lax.rem(row + offset // columns, rows)
+        return there_col, there_row
+
+    def origin(offset):
+        from_col = lax.rem(col + columns - offset % columns, columns)
+        from_row = lax.rem(row + rows - offset // columns, rows)
+        return from_col * rows + from_row
+
+    def greet(offset, carry):
+        pl.semaphore_signal(barrier, inc=1, device_id=target(offset), device_id_type=MESH)
+        return carry
+
+    lax.fori_loop(1, devices, greet, 0)
+    build_north_table(sz, fine_north, coarse_north, table_north)
+    pl.semaphore_wait(barrier, devices - 1)
+
+    def block_of(device):
+        return pl.ds(pl.multiple_of(device * share, share), share)
+
+    def send(chunk, offset, slot_ref):
+        there_col, there_row = target(offset)
+        return pltpu.make_async_remote_copy(
+            src_ref=outgoing.at[chunk, :, block_of(there_col * rows + there_row)],
+            dst_ref=slot_ref,
+            send_sem=send_sem.at[chunk, offset],
+            recv_sem=recv_sem.at[chunk, offset],
+            device_id=(there_col, there_row),
+            device_id_type=MESH,
+        )
+
+    def own(chunk, slot_ref):
+        return pltpu.make_async_copy(outgoing.at[chunk, :, block_of(me)], slot_ref, own_sem.at[chunk])
+
+    def launch(chunk, arrivals):
+        own(chunk, arrivals(me)).start()
+
+        def step(offset, carry):
+            send(chunk, offset, arrivals(me)).start()
+            return carry
+
+        lax.fori_loop(1, devices, step, 0)
+
+    def collect(chunk, arrivals):
+        own(chunk, arrivals(me)).wait()
+
+        def step(offset, carry):
+            send(chunk, offset, arrivals(origin(offset))).wait_recv()
+            return carry
+
+        lax.fori_loop(1, devices, step, 0)
+
+    def drain(chunk, arrivals):
+        def step(offset, carry):
+            send(chunk, offset, arrivals(me)).wait_send()
+            return carry
+
+        lax.fori_loop(1, devices, step, 0)
+
+    def produce(chunk, carry):
+        slot, wind = chunk // 2, chunk % 2
+        @pl.when(wind == 0)
+        def _():
+            def wait_load(strip, inner):
+                for copy in load(slot, strip):
+                    copy.wait()
+                return inner
+
+            lax.fori_loop(0, strips, wait_load, 0)
+
+        build_folded(sz, slot, wind, col, curl, source, cut, twiddle, folded)
+        north_transform(sz, chunk, table_north, folded, outgoing)
+
+        @pl.when(chunk < chunks - 1)
+        def _():
+            launch(chunk, lambda device: incoming.at[chunk, device])
+
+        @pl.when(chunk == chunks - 1)
+        def _():
+            launch(chunk, lambda device: last.at[device])
+
+        return carry
+
+    lax.fori_loop(0, chunks, produce, 0)
+    build_east_table(sz, fine_east, coarse_east, table_east)
+    table_copy = pltpu.make_async_copy(table_east, table_out, table_sem)
+    table_copy.start()
+
+    def result_copy(chunk):
+        return pltpu.make_async_copy(grid, results.at[chunk], out_sem)
+
+    def consume(chunk, carry):
+        collect(chunk, lambda device: incoming.at[chunk, device])
+        build_waves(sz, incoming.at[chunk], waves)
+
+        @pl.when(chunk > 0)
+        def _():
+            result_copy(chunk - 1).wait()
+
+        def tile(index, inner):
+            at = pl.multiple_of(index * 256, 256)
+            total, rest = east_tile(sz, waves, table_east, pl.ds(at, 256))
+            grid[:, pl.ds(at, 256)] = total
+            grid[:, pl.ds(pl.multiple_of(at + cells, 256), 256)] = rest
+            return inner
+
+        lax.fori_loop(0, cells // 256, tile, 0)
+        result_copy(chunk).start()
+        return carry
+
+    lax.fori_loop(0, chunks - 1, consume, 0)
+    result_copy(chunks - 2).wait()
+    table_copy.wait()
+
+    def drain_early(chunk, carry):
+        drain(chunk, lambda device: incoming.at[chunk, device])
+        return carry
+
+    lax.fori_loop(0, chunks - 1, drain_early, 0)
+    collect(chunks - 1, lambda device: last.at[device])
+    drain(chunks - 1, lambda device: last.at[device])
+
+
+def finish_kernel(
+    sz, level_slot, results, last, table, u_wind, v_wind, u_slope, v_slope,
+    arrived, east, waves, grid, stage, arrive_sem, table_sem, stage_sem, place_sem, write_sem,
+):
+    rows, slots, share, cells = sz["rows"], sz["slots"], sz["share"], sz["cells"]
+    chunks = 2 * slots
+    outs = ((u_wind, v_wind), (u_slope, v_slope))
+    tiles = cells // 256
+    arrive = pltpu.make_async_copy(last, arrived, arrive_sem)
+    arrive.start()
+    tables = []
+    for t in range(tiles):
+        at = pl.ds(t * 256, 256)
+        copy = pltpu.make_async_copy(table.at[:, :, :, at], east.at[:, :, :, at], table_sem.at[t])
+        copy.start()
+        tables.append(copy)
+    staged = []
+    for chunk in range(chunks - 1):
+        copy = pltpu.make_async_copy(results.at[chunk], stage.at[chunk], stage_sem.at[chunk])
+        copy.start()
+        staged.append(copy)
+
+    def level_of(row, slot):
+        return level_slot[row * slots + slot]
+
+    pending = []
+
+    def place(chunk):
+        staged[chunk].wait()
+        for kind in range(2):
+            for row in range(rows):
+                lines = pl.ds((kind * rows + row) * share, share)
+                copy = pltpu.make_async_copy(
+                    stage.at[chunk, lines],
+                    outs[kind][chunk % 2].at[level_of(row, chunk // 2)],
+                    place_sem.at[chunk, kind * rows + row],
+                )
+                copy.start()
+                pending.append(copy)
+
+    arrive.wait()
+    build_waves(sz, arrived, waves)
+    for t in range(tiles):
+        tables[t].wait()
+        total, rest = east_tile(sz, waves, east, pl.ds(t * 256, 256))
+        grid[:, t * 256:(t + 1) * 256] = total
+        grid[:, cells + t * 256:cells + (t + 1) * 256] = rest
+        for part, start in enumerate((t * 256, cells + t * 256)):
+            for kind in range(2):
+                for row in range(rows):
+                    lines = pl.ds((kind * rows + row) * share, share)
+                    copy = pltpu.make_async_copy(
+                        grid.at[lines, pl.ds(start, 256)],
+                        outs[kind][1].at[level_of(row, slots - 1), :, pl.ds(start, 256)],
+                        write_sem.at[t, part, kind * rows + row],
+                    )
+                    copy.start()
+                    pending.append(copy)
+        if t < chunks - 1:
+            place(t)
+    for chunk in range(tiles, chunks - 1):
+        place(chunk)
+    for copy in pending:
+        copy.wait()
+
+
+def on_device(vorticity, divergence, trunc_cut, level_slot):
+    columns, row_devices = lax.axis_size("col"), lax.axis_size("row")
+    sz = sizes_of(vorticity.shape, columns, row_devices)
+    if sz["local"] != LANES or sz["cells"] % 256 or sz["quarter"] % LANES:
+        return general_device(vorticity, divergence, trunc_cut, level_slot)
+    local, half, quarter, cells = sz["local"], sz["half"], sz["quarter"], sz["cells"]
+    devices, slots, share, east = sz["devices"], sz["slots"], sz["share"], sz["east"]
+    chunks, levels = 2 * slots, slots * row_devices
+    strips = sz["north"] // LANES
+    lines = 2 * row_devices * share
+    column = np.arange(quarter)
+    fine_north = cos_sin(np.arange(FINE)[:, None] * column, quarter)
+    coarse_north = cos_sin(FINE * np.arange(quarter // FINE)[:, None] * column, quarter)
+    twiddle = cos_sin(np.arange(4)[:, None] * column, sz["north"]).transpose(1, 0, 2).reshape(8, quarter)
+    cell = np.arange(cells)
+    fine_east = cos_sin(2 * np.arange(half)[:, None] * cell, east)
+    first = np.arange(2)[:, None] + local * np.arange(columns)[None, :]
+    coarse_east = cos_sin(first.reshape(-1, 1) * cell, east)
+    cut = jnp.broadcast_to(trunc_cut[:, None], (local, LANES))
+    f32, bf16 = jnp.float32, jnp.bfloat16
+    anywhere = pl.BlockSpec(memory_space=pl.ANY)
+    here = pl.BlockSpec(memory_space=pltpu.VMEM)
+    results, last, table = pl.pallas_call(
+        functools.partial(exchange_kernel, sz),
+        out_shape=(
+            jax.ShapeDtypeStruct((chunks - 1, lines, east), f32),
+            jax.ShapeDtypeStruct((devices, 2, share, local), f32),
+            jax.ShapeDtypeStruct((2, 2, cells, cells), bf16),
+        ),
+        in_specs=[anywhere] * 2 + [here] * 6,
+        out_specs=(anywhere,) * 3,
+        scratch_shapes=[
+            pltpu.VMEM((slots, strips, 2, local, LANES), f32),
+            pltpu.VMEM((slots, strips, 2, local, LANES), f32),
+            pltpu.VMEM((2, quarter, 2 * quarter), bf16),
+            pltpu.VMEM((2, 2, cells, cells), bf16),
+            pltpu.VMEM((2, 4, 2 * local, 2 * quarter), bf16),
+            pltpu.VMEM((chunks, 2, sz["north"], local), f32),
+            pltpu.VMEM((chunks - 1, devices, 2, share, local), f32),
+            pltpu.VMEM((2, 2, lines, cells), bf16),
+            pltpu.VMEM((lines, east), f32),
+            pltpu.SemaphoreType.DMA((2, slots, strips)),
+            pltpu.SemaphoreType.DMA((chunks, devices)),
+            pltpu.SemaphoreType.DMA((chunks, devices)),
+            pltpu.SemaphoreType.DMA((chunks,)),
+            pltpu.SemaphoreType.DMA,
+            pltpu.SemaphoreType.DMA,
+        ],
+        compiler_params=pltpu.CompilerParams(
+            collective_id=0, has_side_effects=True, vmem_limit_bytes=60 * 1024 * 1024
+        ),
+        name="exchange",
+    )(vorticity, divergence, cut, fine_north, coarse_north, twiddle, fine_east, coarse_east)
+    out = jax.ShapeDtypeStruct((levels, share, east), f32)
+    return pl.pallas_call(
+        functools.partial(finish_kernel, sz),
+        out_shape=(out,) * 4,
+        in_specs=[pl.BlockSpec(memory_space=pltpu.SMEM)] + [anywhere] * 3,
+        out_specs=(anywhere,) * 4,
+        scratch_shapes=[
+            pltpu.VMEM((devices, 2, share, local), f32),
+            pltpu.VMEM((2, 2, cells, cells), bf16),
+            pltpu.VMEM((2, 2, lines, cells), bf16),
+            pltpu.VMEM((lines, east), f32),
+            pltpu.VMEM((chunks - 1, lines, east), f32),
+            pltpu.SemaphoreType.DMA,
+            pltpu.SemaphoreType.DMA((cells // 256,)),
+            pltpu.SemaphoreType.DMA((chunks - 1,)),
+            pltpu.SemaphoreType.DMA((chunks - 1, 2 * row_devices)),
+            pltpu.SemaphoreType.DMA((cells // 256, 2, 2 * row_devices)),
+        ],
+        compiler_params=pltpu.CompilerParams(vmem_limit_bytes=60 * 1024 * 1024),
+        name="finish",
+    )(level_slot, results, last, table)
+
+
 def solution(mesh):
     return jax.shard_map(
         on_device,
         mesh=mesh,
         in_specs=(P(None, "row", "col", None), P(None, "row", "col", None), P("col"), P()),
-        out_specs=(
-            P(None, ("col", "row"), None),
-            P(None, ("col", "row"), None),
-            P(None, ("col", "row"), None),
-            P(None, ("col", "row"), None),
-        ),
+        out_specs=(P(None, ("col", "row"), None),) * 4,
         check_vma=False,
     )

time: 373 us -> 218 us (0.58)
  Pallas kernels: 0 us -> 213 us
  local copies, waits for them, and re-layouts: 109 us -> 1.37 us
  waiting for transfers between devices: 102 us -> 0 us
  matrix products: 66.9 us -> 0 us
  other arithmetic: 59 us -> 0 us
  between operations: 16.5 us -> 0.64 us
  starting transfers between devices: 14 us -> 0 us
    pallas_call x0 -> x2, Pallas kernels: none -> 213 us  [the longest x1 196 us: on_device(): pl.pallas_call(functools.partial(exchange_kernel, sz), out_shape=(jax.Sha...]
    all_to_all x2 -> x0, waiting for transfers between devices: 102 us -> none  [on_device(): lax.all_to_all(outgoing, ('col', 'row'), split_axis=0, concat_axis=0, til...]
    dot_general x6 -> x0, matrix products: 66.9 us -> none  [the longest x2 28.6 us: on_device(): fourier = jnp.einsum('pjk,pmk->pjm', table_north, folded, precision=HIGH)]
    slice x13 -> x0, local copies, waits for them, and re-layouts: 44.7 us -> none  [the longest x4 20.8 us: split_waves(): first = lax.slice_in_dim(array, 0, None, 2, axis)]
    reshape x6 -> x0, local copies, waits for them, and re-layouts: 33.2 us -> none  [the longest x2 12.5 us: on_device(): received.reshape(columns, row_devices, block, slots, 4, 2, local_waves)]
    concatenate x21 -> x0, other arithmetic: 24.1 us -> none  [the longest x8 11.9 us: fold_quarters(): parts.append(jnp.concatenate([top, low], axis=2))]
    unnamed x70 -> x0, local copies, waits for them, and re-layouts: 17.4 us -> none
    another operation x2 -> x0, other arithmetic: 16.2 us -> none  [east_table(): joined = jnp.stack([real, imag], axis=2)]
  transfers between devices with their start and end apart: 2 -> 0, of which waited for: 2 -> 0; matrix products, arithmetic and copies ran while one was open for 19% -> 0% of each run, Pallas kernels for 0% -> 0%
where the time goes in v1:
time: 218 us; the launch traced here: 215 us
  Pallas kernels  213 us (98%)
    pallas_call x1, Pallas kernels, on_device(): pl.pallas_call(functools.partial(exchange_kernel, sz), out_shape=(jax.Sha...  196 us
    pallas_call x1, Pallas kernels, on_device(): pl.pallas_call(functools.partial(finish_kernel, sz), out_shape=(out,) * 4...  17 us

profile of v1, /device:TPU:1, one launch (start us, length us, event | category | flops | bytes accessed | tf_op | source)
XLA Modules:
  0.0 215.1 jit_solution(13089087173663933535)
XLA Ops:
  0.6 1.4 broadcast_in_dim.2.cut
  2.0 196.0 %exchange.1 = (f32[3,512,2048]{2,1,0:T(8,128)}, f32[32,2,64,128]{3,2,1,0:T(8,128)}, bf16[2,2,1024,1024]{3,2,1,0:T(8,128)(2,1)}) custom-call(f32[2,2,128,2048]{3,2,1,0:T(8,128)} %curl_hbm.1, f32[2,2,128,2048]{3,2,1,0:T(8,128)} %source_hbm.1, s32[128,128]{1,0:T(8,128)} %broadcast_in_dim.2.cut, f32[2,32,512]{2,1,0:T(8,128)} %constant.10.clone.fine_north, ...), custom_call_target="tpu_custom_call" | custom-call | tf_op jit(solution)/shard_map/exchange/pallas_call | solution.py:570
  198.0 17.0 %finish.1 = (f32[8,64,2048]{2,1,0:T(8,128)}, f32[8,64,2048]{2,1,0:T(8,128)}, f32[8,64,2048]{2,1,0:T(8,128)}, f32[8,64,2048]{2,1,0:T(8,128)}) custom-call(s32[8]{0:T(128)} %level_slot.1, f32[3,512,2048]{2,1,0:T(8,128)} %get-tuple-element.7.results, f32[32,2,64,128]{3,2,1,0:T(8,128)} %get-tuple-element.8.last, bf16[2,2,1024,1024]{3,2,1,0:T(8,128)(2,1)} %get-tuple-element.9.table), custom_call_target="tpu_custom_call" | custom-call | tf_op jit(solution)/shard_map/finish/pallas_call | solution.py:602

commit v2 on v1

v2 whole, which is shorter than its diff:
```python
import functools
import math

import jax
import jax.numpy as jnp
import numpy as np
from jax import lax
from jax.experimental import pallas as pl
from jax.experimental.pallas import tpu as pltpu
from jax.sharding import PartitionSpec as P

MESH = pl.DeviceIdType.MESH
LANES = 128
ROWS = 16
FINE = 32
TILE = 256
HIGH = lax.Precision.HIGH


def split_waves(array, axis):
    first = lax.slice_in_dim(array, 0, None, 2, axis)
    second = lax.slice_in_dim(array, 1, None, 2, axis)
    return jnp.concatenate([first, second], axis)


def phases(product, period):
    angles = 2.0 * np.pi * (product % period) / period
    return np.cos(angles).astype(np.float32), np.sin(angles).astype(np.float32)


def multiply(first, second):
    return first[0] * second[0] - first[1] * second[1], first[0] * second[1] + first[1] * second[0]


def north_table(north_cells):
    quarter = north_cells // 4
    fine = math.gcd(quarter, 32)
    column = np.arange(quarter)
    coarse_row = 4 * fine * np.arange(quarter // fine)[None, :, None, None] + np.arange(4)[:, None, None, None]
    fine_row = 4 * np.arange(fine)[None, None, :, None]
    coarse = phases(coarse_row * column, north_cells)
    close = phases(fine_row * column, north_cells)
    coarse, close = lax.optimization_barrier((coarse, close))
    cosine, sine = multiply(coarse, close)
    joined = jnp.concatenate([cosine, -sine], axis=3)
    return joined.reshape(4, quarter, 2 * quarter)


def east_table(columns, local_waves, east_cells):
    half = local_waves // 2
    cells = east_cells // 2
    column = np.arange(cells)
    coarse_wave = np.arange(2)[:, None, None, None] + local_waves * np.arange(columns)[None, :, None, None]
    close_wave = 2 * np.arange(half)[None, None, :, None]
    coarse = phases(coarse_wave * column, east_cells)
    close = phases(close_wave * column, east_cells)
    coarse, close = lax.optimization_barrier((coarse, close))
    cosine, sine = multiply(coarse, close)
    wave = coarse_wave + close_wave
    weights = np.where(wave == 0, 1.0, 2.0).astype(np.float32)
    scaled = (weights * wave * (2.0 * np.pi / east_cells)).astype(np.float32)
    real = jnp.concatenate([weights * cosine, -scaled * sine], axis=3)
    imag = jnp.concatenate([-weights * sine, -scaled * cosine], axis=3)
    joined = jnp.stack([real, imag], axis=2)
    return joined.reshape(2, columns * local_waves, 2 * cells)


def spectral_winds(vorticity, divergence, trunc_cut, wave_index, east_cells):
    north_cells = vorticity.shape[3]
    north_index = jnp.arange(north_cells, dtype=jnp.int32)
    north_wave = jnp.where(north_index < north_cells // 2, north_index, north_index - north_cells)
    wave_east = 2.0 * math.pi / east_cells * wave_index.astype(jnp.float32)
    wave_north = 2.0 * math.pi / north_cells * north_wave.astype(jnp.float32)
    east_col = wave_east[:, None]
    north_row = wave_north[None, :]
    square_wave = east_col * east_col + north_row * north_row
    retained = (jnp.abs(north_wave)[None, :] <= trunc_cut[:, None]) & (square_wave > 0)
    inverse_square = jnp.where(retained, 1.0 / jnp.where(square_wave > 0, square_wave, 1.0), 0.0)
    east_inverse = east_col * inverse_square
    north_inverse = north_row * inverse_square
    curl_real, curl_imag = vorticity[0], vorticity[1]
    source_real, source_imag = divergence[0], divergence[1]
    east = (
        -north_inverse * curl_imag + east_inverse * source_imag,
        north_inverse * curl_real - east_inverse * source_real,
    )
    north = (
        east_inverse * curl_imag + north_inverse * source_imag,
        -east_inverse * curl_real - north_inverse * source_real,
    )
    return east, north


def fold_quarters(wind, slots, half):
    real, imag = wind
    quarter = real.shape[2] // 4
    r0, r1, r2, r3 = (real[:, :, q * quarter:(q + 1) * quarter] for q in range(4))
    i0, i1, i2, i3 = (imag[:, :, q * quarter:(q + 1) * quarter] for q in range(4))
    folded = (
        (r0 + r2 + (r1 + r3), i0 + i2 + (i1 + i3)),
        (r0 - r2 - (i1 - i3), i0 - i2 + (r1 - r3)),
        (r0 + r2 - (r1 + r3), i0 + i2 - (i1 + i3)),
        (r0 - r2 + (i1 - i3), i0 - i2 - (r1 - r3)),
    )
    parts = []
    for part_real, part_imag in folded:
        shape = (slots, 2, 1, half, 2 * quarter)
        top = jnp.concatenate([part_real, part_imag], axis=2).reshape(shape)
        low = jnp.concatenate([part_imag, -part_real], axis=2).reshape(shape)
        parts.append(jnp.concatenate([top, low], axis=2))
    return jnp.stack(parts, axis=0).reshape(4, slots * 4 * half, 2 * quarter)


def general_device(vorticity, divergence, trunc_cut, level_slot):
    columns = lax.axis_size("col")
    row_devices = lax.axis_size("row")
    slots, local_waves, north_cells = vorticity.shape[1:]
    half = local_waves // 2
    quarter = north_cells // 4
    levels = slots * row_devices
    east_cells = 2 * local_waves * columns
    cells = east_cells // 2
    block = quarter // (columns * row_devices)
    first_wave = lax.axis_index("col") * local_waves
    wave_index = first_wave + jnp.arange(local_waves, dtype=jnp.int32)
    winds = spectral_winds(
        split_waves(vorticity, 2),
        split_waves(divergence, 2),
        split_waves(trunc_cut, 0),
        split_waves(wave_index, 0),
        east_cells,
    )
    table_north = north_table(north_cells)
    table_east = east_table(columns, local_waves, east_cells)
    holder = jnp.argsort(level_slot).astype(jnp.int32)
    results = []
    for wind in winds:
        folded = fold_quarters(wind, slots, half)
        fourier = jnp.einsum("pjk,pmk->pjm", table_north, folded, precision=HIGH)
        outgoing = fourier.reshape(4, quarter, slots, 2 * local_waves).transpose(1, 2, 0, 3)
        received = lax.all_to_all(outgoing, ("col", "row"), split_axis=0, concat_axis=0, tiled=True)
        shaped = received.reshape(columns, row_devices, block, slots, 4, 2, local_waves)
        arranged = shaped.transpose(1, 3, 5, 2, 4, 0, 6).reshape(
            levels, 2, block * 4, columns * local_waves
        )
        placed = jnp.concatenate(
            [lax.dynamic_slice_in_dim(arranged, holder[level], 1, 0) for level in range(levels)], axis=0
        )
        even = jnp.einsum("lyk,kx->lyx", placed[:, 0], table_east[0], precision=HIGH)
        odd = jnp.einsum("lyk,kx->lyx", placed[:, 1], table_east[1], precision=HIGH)
        total, rest = even + odd, even - odd
        results.append(
            (
                jnp.concatenate([total[:, :, :cells], rest[:, :, :cells]], axis=2),
                jnp.concatenate([total[:, :, cells:], rest[:, :, cells:]], axis=2),
            )
        )
    return results[0][0], results[1][0], results[0][1], results[1][1]


def cos_sin(product, period):
    angles = 2.0 * np.pi * (product % period) / period
    return np.stack([np.cos(angles), np.sin(angles)]).astype(np.float32)


def split(value):
    high = value.astype(jnp.bfloat16)
    return high, (value - high.astype(jnp.float32)).astype(jnp.bfloat16)


def dot3(left, right, dims):
    def one(first, second):
        return lax.dot_general(first, second, (dims, ((), ())), preferred_element_type=jnp.float32)

    return one(left[0], right[0]) + one(left[0], right[1]) + one(left[1], right[0])


def sizes_of(shape, columns, row_devices):
    slots, local, north_cells = shape[1:]
    return dict(
        columns=columns,
        rows=row_devices,
        devices=columns * row_devices,
        slots=slots,
        local=local,
        half=local // 2,
        north=north_cells,
        quarter=north_cells // 4,
        share=north_cells // (columns * row_devices),
        east=2 * local * columns,
        cells=local * columns,
    )


def build_north_table(sz, fine, coarse, table):
    quarter = sz["quarter"]

    def step(g, carry):
        cos_c, sin_c = coarse[0, pl.ds(g, 1), :], coarse[1, pl.ds(g, 1), :]
        cos_f, sin_f = fine[0], fine[1]
        cosine = cos_c * cos_f - sin_c * sin_f
        sine = -(sin_c * cos_f + cos_c * sin_f)
        at = pl.ds(pl.multiple_of(g * FINE, FINE), FINE)
        for part, value in ((0, cosine), (1, sine)):
            high, low = split(value)
            table[0, at, part * quarter:(part + 1) * quarter] = high
            table[1, at, part * quarter:(part + 1) * quarter] = low
        return carry

    lax.fori_loop(0, quarter // FINE, step, 0)


def build_east_table(sz, parity, fine, coarse, table):
    half, columns, cells = sz["half"], sz["columns"], sz["cells"]

    def step(column, carry):
        base = column * (2 * half)
        index = parity * columns + column
        for start in range(0, cells, TILE):
            lanes = slice(start, start + TILE)
            cos_c, sin_c = coarse[0, pl.ds(index, 1), lanes], coarse[1, pl.ds(index, 1), lanes]
            cos_f, sin_f = fine[0, :, lanes], fine[1, :, lanes]
            cosine = cos_c * cos_f - sin_c * sin_f
            sine = -(sin_c * cos_f + cos_c * sin_f)
            for part, value in ((0, cosine), (1, sine)):
                at = pl.ds(pl.multiple_of(base + part * half, half), half)
                high, low = split(value)
                table[0, at, lanes] = high
                table[1, at, lanes] = low
        return carry

    lax.fori_loop(0, columns, step, 0)


def build_folded(sz, slot, wind, parity, column, curl, source, cut, twiddle, folded, ready):
    half, quarter, north = sz["half"], sz["quarter"], sz["north"]
    is_north = wind == 1

    def step(block, carry):
        ready(block)
        lanes = pl.multiple_of(block * LANES, LANES)
        index = lax.broadcasted_iota(jnp.int32, (ROWS, LANES), 1) + lanes
        line = lax.broadcasted_iota(jnp.int32, (ROWS, LANES), 0)
        for top in range(0, half, ROWS):
            at = pl.ds(parity + 2 * top, ROWS, stride=2)
            wave = column * (2 * half) + parity + 2 * (line + top)
            kx = (2.0 * math.pi / sz["east"]) * wave.astype(jnp.float32)
            weight = jnp.where(wave == 0, 1.0, 2.0)
            kept = cut[at, :]
            real, imag = [], []
            for q in range(4):
                number = index + q * quarter
                number = jnp.where(number < north // 2, number, number - north)
                ky = (2.0 * math.pi / north) * number.astype(jnp.float32)
                square = kx * kx + ky * ky
                retained = (jnp.abs(number) <= kept) & (square > 0)
                inverse = jnp.where(retained, weight / jnp.where(square > 0, square, 1.0), 0.0)
                by_x, by_y = kx * inverse, ky * inverse
                first = jnp.where(is_north, by_x, -by_y)
                second = jnp.where(is_north, by_y, by_x)
                strip = block + q * (quarter // LANES)
                zr, zi = curl[slot, strip, 0, at, :], curl[slot, strip, 1, at, :]
                dr, di = source[slot, strip, 0, at, :], source[slot, strip, 1, at, :]
                real.append(first * zi + second * di)
                imag.append(-(first * zr + second * dr))
            (r0, r1, r2, r3), (i0, i1, i2, i3) = real, imag
            rs, rd, rt, ru = r0 + r2, r0 - r2, r1 + r3, r1 - r3
            js, jd, jt, ju = i0 + i2, i0 - i2, i1 + i3, i1 - i3
            parts = ((rs + rt, js + jt), (rd - ju, jd + ru), (rs - rt, js - jt), (rd + ju, jd - ru))
            near = pl.ds(lanes, LANES)
            far = pl.ds(pl.multiple_of(lanes + quarter, LANES), LANES)
            for p, (a, b) in enumerate(parts):
                if p:
                    cosine = twiddle[2 * p:2 * p + 1, near]
                    sine = twiddle[2 * p + 1:2 * p + 2, near]
                    a, b = a * cosine - b * sine, a * sine + b * cosine
                upper = slice(p * 2 * half + top, p * 2 * half + top + ROWS)
                lower = slice(p * 2 * half + half + top, p * 2 * half + half + top + ROWS)
                for level, (x, y) in enumerate(zip(split(a), split(b))):
                    folded[level, upper, near] = x
                    folded[level, upper, far] = y
                    folded[level, lower, near] = y
                    folded[level, lower, far] = -x
        return carry

    lax.fori_loop(0, quarter // LANES, step, 0)


def north_transform(sz, chunk, table, folded, outgoing):
    quarter, pair = sz["quarter"], 2 * LANES
    for p in range(0, 4, 2):
        rows = slice(p * LANES, p * LANES + pair)
        sums = dot3((table[0], table[1]), (folded[0, rows], folded[1, rows]), ((1,), (1,)))
        outgoing[chunk, pl.ds(p, quarter, stride=4), :] = sums[:, :LANES]
        outgoing[chunk, pl.ds(p + 1, quarter, stride=4), :] = sums[:, LANES:]


def build_waves(sz, parity, received, waves):
    columns, half = sz["columns"], sz["half"]
    lines = sz["rows"] * sz["share"]

    def step(column, carry):
        sources = pl.ds(pl.multiple_of(column * sz["rows"], sz["rows"]), sz["rows"])
        lane = lax.broadcasted_iota(jnp.int32, (1, 2 * half), 1)
        into = pl.ds(pl.multiple_of(column * 2 * half, LANES), 2 * half)
        value = received[sources].reshape(lines, 2 * half)
        wave = column * (2 * half) + parity + 2 * jnp.where(lane < half, lane, lane - half)
        kx = (2.0 * math.pi / sz["east"]) * wave.astype(jnp.float32)
        slope = pltpu.roll(value, half, axis=1) * jnp.where(lane < half, -kx, kx)
        for kind, data in enumerate((value, slope)):
            high, low = split(data)
            waves[0, kind * lines:(kind + 1) * lines, into] = high
            waves[1, kind * lines:(kind + 1) * lines, into] = low
        return carry

    lax.fori_loop(0, columns, step, 0)


def east_tile(waves, table, lanes):
    return dot3((waves[0], waves[1]), (table[0, :, lanes], table[1, :, lanes]), ((1,), (0,)))


def exchange_kernel(
    sz, curl_hbm, source_hbm, cut_row, fine_north, coarse_north, twiddle, fine_east, coarse_east,
    results, even, last, table_odd,
    curl, source, cut, table_north, table_even, folded, outgoing, incoming, waves,
    load_sem, send_sem, recv_sem, own_sem,
):
    columns, rows, devices, slots = sz["columns"], sz["rows"], sz["devices"], sz["slots"]
    share, cells, quarter = sz["share"], sz["cells"], sz["quarter"]
    chunks = 4 * slots
    col, row = lax.axis_index("col"), lax.axis_index("row")
    me = col * rows + row
    blocks = quarter // LANES
    strips = 4 * blocks

    def load(slot, strip):
        lanes = pl.ds(pl.multiple_of(strip * LANES, LANES), LANES)
        for which, (hbm, near) in enumerate(((curl_hbm, curl), (source_hbm, source))):
            yield pltpu.make_async_copy(
                hbm.at[:, slot, :, lanes], near.at[slot, strip], load_sem.at[which, slot, strip]
            )

    def start_load(index, carry):
        turn = index % strips
        for copy in load(index // strips, (turn % 4) * blocks + turn // 4):
            copy.start()
        return carry

    lax.fori_loop(0, slots * strips, start_load, 0)
    barrier = pltpu.get_barrier_semaphore()
    itself = columns // 2

    def target(offset):
        there_col = lax.rem(col + itself + offset % columns, columns)
        there_row = lax.rem(row + offset // columns, rows)
        return there_col, there_row

    def origin(offset):
        from_col = lax.rem(col + 2 * columns - itself - offset % columns, columns)
        from_row = lax.rem(row + rows - offset // columns, rows)
        return from_col * rows + from_row

    def others(step):
        lax.fori_loop(0, itself, step, 0)
        lax.fori_loop(itself + 1, devices, step, 0)

    def greet(offset, carry):
        pl.semaphore_signal(barrier, inc=1, device_id=target(offset), device_id_type=MESH)
        return carry

    others(greet)
    cut[...] = jnp.broadcast_to(cut_row[...], (sz["local"], sz["local"])).T
    build_north_table(sz, fine_north, coarse_north, table_north)

    def block_of(device):
        return pl.ds(pl.multiple_of(device * share, share), share)

    def send(chunk, offset, slot_ref):
        there_col, there_row = target(offset)
        return pltpu.make_async_remote_copy(
            src_ref=outgoing.at[chunk, block_of(there_col * rows + there_row)],
            dst_ref=slot_ref,
            send_sem=send_sem.at[chunk, offset],
            recv_sem=recv_sem.at[chunk, offset],
            device_id=(there_col, there_row),
            device_id_type=MESH,
        )

    def own(chunk, slot_ref):
        return pltpu.make_async_copy(outgoing.at[chunk, block_of(me)], slot_ref, own_sem.at[chunk])

    def launch(chunk, arrivals):
        def step(offset, carry):
            send(chunk, offset, arrivals(me)).start()
            return carry

        others(step)
        own(chunk, arrivals(me)).start()

    def collect(chunk, arrivals):
        own(chunk, arrivals(me)).wait()

        def step(offset, carry):
            send(chunk, offset, arrivals(origin(offset))).wait_recv()
            return carry

        others(step)

    def drain(chunk, arrivals):
        def step(offset, carry):
            send(chunk, offset, arrivals(me)).wait_send()
            return carry

        others(step)

    def produce(chunk, carry):
        slot, wind, parity = chunk // 4, (chunk // 2) % 2, chunk % 2

        def ready(block):
            @pl.when(chunk % 4 == 0)
            def _():
                for q in range(4):
                    for copy in load(slot, block + q * blocks):
                        copy.wait()

        build_folded(sz, slot, wind, parity, col, curl, source, cut, twiddle, folded, ready)
        north_transform(sz, chunk, table_north, folded, outgoing)

        @pl.when(chunk == 0)
        def _():
            pl.semaphore_wait(barrier, devices - 1)

        @pl.when(chunk < chunks - 1)
        def _():
            launch(chunk, lambda device: incoming.at[chunk, device])

        @pl.when(chunk == chunks - 1)
        def _():
            launch(chunk, lambda device: last.at[device])

        return carry

    lax.fori_loop(0, chunks, produce, 0)
    build_east_table(sz, 0, fine_east, coarse_east, table_even)
    build_east_table(sz, 1, fine_east, coarse_east, table_odd)

    def consume(chunk, carry):
        collect(chunk, lambda device: incoming.at[chunk, device])
        pair, parity = chunk // 2, chunk % 2
        build_waves(sz, parity, incoming.at[chunk], waves)

        @pl.when(parity == 0)
        def _():
            def tile(index, inner):
                at = pl.ds(pl.multiple_of(index * TILE, TILE), TILE)
                even[:, at] = east_tile(waves, table_even, at)
                return inner

            lax.fori_loop(0, cells // TILE, tile, 0)

        @pl.when(parity == 1)
        def _():
            def tile(index, inner):
                at = pl.ds(pl.multiple_of(index * TILE, TILE), TILE)
                beyond = pl.ds(pl.multiple_of(index * TILE + cells, TILE), TILE)
                odd = east_tile(waves, table_odd, at)
                results[pair, :, at] = even[:, at] + odd
                results[pair, :, beyond] = even[:, at] - odd
                return inner

            lax.fori_loop(0, cells // TILE, tile, 0)

        return carry

    lax.fori_loop(0, chunks - 1, consume, 0)

    def drain_early(chunk, carry):
        drain(chunk, lambda device: incoming.at[chunk, device])
        return carry

    lax.fori_loop(0, chunks - 1, drain_early, 0)
    drain(chunks - 1, lambda device: last.at[device])
    collect(chunks - 1, lambda device: last.at[device])


def finish_kernel(
    sz, level_slot, results, even, last, table_odd, u_wind, v_wind, u_slope, v_slope,
    waves, grid, place_sem, write_sem,
):
    rows, slots, share, cells = sz["rows"], sz["slots"], sz["share"], sz["cells"]
    pairs = 2 * slots
    outs = ((u_wind, v_wind), (u_slope, v_slope))
    pending = []
    spots = [(kind, row) for kind in range(2) for row in range(rows)]

    def spread(source_ref, pair, lanes, sems):
        for index, (kind, row) in enumerate(spots):
            lines = pl.ds(index * share, share)
            level = level_slot[row * slots + pair // 2]
            copy = pltpu.make_async_copy(
                source_ref.at[lines, lanes], outs[kind][pair % 2].at[level, :, lanes], sems.at[index]
            )
            copy.start()
            pending.append(copy)

    for pair in range(pairs - 1):
        spread(results.at[pair], pair, pl.ds(0, 2 * cells), place_sem.at[pair])
    build_waves(sz, 1, last, waves)
    for t in range(cells // TILE):
        odd = east_tile(waves, table_odd, pl.ds(t * TILE, TILE))
        held = even[:, t * TILE:(t + 1) * TILE]
        for part, value in enumerate((held + odd, held - odd)):
            start = part * cells + t * TILE
            grid[:, start:start + TILE] = value
            spread(grid, pairs - 1, pl.ds(start, TILE), write_sem.at[t, part])
    for copy in pending:
        copy.wait()


def on_device(vorticity, divergence, trunc_cut, level_slot):
    columns, row_devices = lax.axis_size("col"), lax.axis_size("row")
    sz = sizes_of(vorticity.shape, columns, row_devices)
    if sz["local"] != LANES or sz["cells"] % 256 or sz["quarter"] % LANES:
        return general_device(vorticity, divergence, trunc_cut, level_slot)
    local, half, quarter, cells = sz["local"], sz["half"], sz["quarter"], sz["cells"]
    devices, slots, share, east = sz["devices"], sz["slots"], sz["share"], sz["east"]
    pairs, chunks, levels = 2 * slots, 4 * slots, slots * row_devices
    strips = sz["north"] // LANES
    lines = 2 * row_devices * share
    column = np.arange(quarter)
    fine_north = cos_sin(np.arange(FINE)[:, None] * column, quarter)
    coarse_north = cos_sin(FINE * np.arange(quarter // FINE)[:, None] * column, quarter)
    twiddle = cos_sin(np.arange(4)[:, None] * column, sz["north"]).transpose(1, 0, 2).reshape(8, quarter)
    cell = np.arange(cells)
    fine_east = cos_sin(2 * np.arange(half)[:, None] * cell, east)
    first = np.arange(2)[:, None] + local * np.arange(columns)[None, :]
    coarse_east = cos_sin(first.reshape(-1, 1) * cell, east)
    f32, bf16 = jnp.float32, jnp.bfloat16
    anywhere = pl.BlockSpec(memory_space=pl.ANY)
    here = pl.BlockSpec(memory_space=pltpu.VMEM)
    results, even, last, table_odd = pl.pallas_call(
        functools.partial(exchange_kernel, sz),
        out_shape=(
            pltpu.VMEM((pairs - 1, lines, east), f32),
            pltpu.VMEM((lines, cells), f32),
            pltpu.VMEM((devices, share, local), f32),
            pltpu.VMEM((2, cells, cells), bf16),
        ),
        in_specs=[anywhere] * 2 + [here] * 6,
        out_specs=(here,) * 4,
        scratch_shapes=[
            pltpu.VMEM((slots, strips, 2, local, LANES), f32),
            pltpu.VMEM((slots, strips, 2, local, LANES), f32),
            pltpu.VMEM((local, LANES), jnp.int32),
            pltpu.VMEM((2, quarter, 2 * quarter), bf16),
            pltpu.VMEM((2, cells, cells), bf16),
            pltpu.VMEM((2, 4 * local, 2 * quarter), bf16),
            pltpu.VMEM((chunks, sz["north"], local), f32),
            pltpu.VMEM((chunks - 1, devices, share, local), f32),
            pltpu.VMEM((2, lines, cells), bf16),
            pltpu.SemaphoreType.DMA((2, slots, strips)),
            pltpu.SemaphoreType.DMA((chunks, devices)),
            pltpu.SemaphoreType.DMA((chunks, devices)),
            pltpu.SemaphoreType.DMA((chunks,)),
        ],
        compiler_params=pltpu.CompilerParams(
            collective_id=0, has_side_effects=True, vmem_limit_bytes=40 * 2**20
        ),
        name="exchange",
    )(
        vorticity, divergence, trunc_cut.reshape(1, local),
        fine_north, coarse_north, twiddle, fine_east, coarse_east,
    )
    out = jax.ShapeDtypeStruct((levels, share, east), f32)
    return pl.pallas_call(
        functools.partial(finish_kernel, sz),
        out_shape=(out,) * 4,
        in_specs=[pl.BlockSpec(memory_space=pltpu.SMEM)] + [here] * 4,
        out_specs=(anywhere,) * 4,
        scratch_shapes=[
            pltpu.VMEM((2, lines, cells), bf16),
            pltpu.VMEM((lines, east), f32),
            pltpu.SemaphoreType.DMA((pairs - 1, 2 * row_devices)),
            pltpu.SemaphoreType.DMA((cells // TILE, 2, 2 * row_devices)),
        ],
        compiler_params=pltpu.CompilerParams(vmem_limit_bytes=16 * 2**20),
        name="finish",
    )(level_slot, results, even, last, table_odd)


def solution(mesh):
    return jax.shard_map(
        on_device,
        mesh=mesh,
        in_specs=(P(None, "row", "col", None), P(None, "row", "col", None), P("col"), P()),
        out_specs=(P(None, ("col", "row"), None),) * 4,
        check_vma=False,
    )
```

time: 218 us -> 205 us (0.940); the launches traced: 215 us -> 205 us
  Pallas kernels: 213 us -> 204 us
    pallas_call x1, Pallas kernels: 17 us -> 7.24 us  [on_device(): pl.pallas_call(functools.partial(finish_kernel, sz), out_shape=(out,) * 4...]
where the time goes in v2:
time: 205 us
  Pallas kernels  204 us (100%)
    pallas_call x1, Pallas kernels, on_device(): pl.pallas_call(functools.partial(exchange_kernel, sz), out_shape=(pltpu.V...  197 us
    pallas_call x1, Pallas kernels, on_device(): pl.pallas_call(functools.partial(finish_kernel, sz), out_shape=(out,) * 4...  7.24 us

profile of v2, /device:TPU:1, one launch (start us, length us, event | category | flops | bytes accessed | tf_op | source)
XLA Modules:
  0.0 204.9 jit_solution(16360138800242316766)
XLA Ops:
  0.6 0.0 copy-start
  0.6 197.0 %exchange.1 = (f32[3,512,2048]{2,1,0:T(8,128)S(1)}, f32[512,1024]{1,0:T(8,128)S(1)}, f32[32,64,128]{2,1,0:T(8,128)S(1)}, bf16[2,1024,1024]{2,1,0:T(8,128)(2,1)S(1)}) custom-call(f32[2,2,128,2048]{3,2,1,0:T(8,128)} %curl_hbm.1, f32[2,2,128,2048]{3,2,1,0:T(8,128)} %source_hbm.1, s32[1,128]{1,0:T(1,128)} %bitcast.1, f32[2,32,512]{2,1,0:T(8,128)} %constant.10.clone.fine_north, ...), custom_call_target="tpu_custom_call" | custom-call | tf_op jit(solution)/shard_map/exchange/pallas_call | solution.py:542
  197.6 0.0 copy-done
  197.7 7.2 %finish.1 = (f32[8,64,2048]{2,1,0:T(8,128)}, f32[8,64,2048]{2,1,0:T(8,128)}, f32[8,64,2048]{2,1,0:T(8,128)}, f32[8,64,2048]{2,1,0:T(8,128)}) custom-call(s32[8]{0:T(128)S(1)} %copy-done, f32[3,512,2048]{2,1,0:T(8,128)S(1)} %get-tuple-element.8.results, f32[512,1024]{1,0:T(8,128)S(1)} %get-tuple-element.9.even, f32[32,64,128]{2,1,0:T(8,128)S(1)} %get-tuple-element.10.last, ...), custom_call_target="tpu_custom_call" | custom-call | tf_op jit(solution)/shard_map/finish/pallas_call | solution.py:576
Async XLA Ops:
  0.6 197.0 %copy-start = (s32[8]{0:T(128)S(1)}, s32[8]{0:T(128)}, u32[]{:S(2)}) copy-start(s32[8]{0:T(128)} %level_slot.1) | copy-start | bytes 100

commit v3 on v2

--- a/solution.py
+++ b/solution.py
@@ -321,10 +321,10 @@
 
 
 def exchange_kernel(
-    sz, curl_hbm, source_hbm, cut_row, fine_north, coarse_north, twiddle, fine_east, coarse_east,
+    sz, curl_hbm, source_hbm, cut_row, fine_north, coarse_north, twiddle, fine_hbm, coarse_hbm,
     results, even, last, table_odd,
-    curl, source, cut, table_north, table_even, folded, outgoing, incoming, waves,
-    load_sem, send_sem, recv_sem, own_sem,
+    curl, source, cut, table_north, table_even, folded, outgoing, incoming, waves, fine_east, coarse_east,
+    load_sem, send_sem, recv_sem, own_sem, phase_sem,
 ):
     columns, rows, devices, slots = sz["columns"], sz["rows"], sz["devices"], sz["slots"]
     share, cells, quarter = sz["share"], sz["cells"], sz["quarter"]
@@ -347,29 +347,32 @@
             copy.start()
         return carry
 
-    lax.fori_loop(0, slots * strips, start_load, 0)
     barrier = pltpu.get_barrier_semaphore()
-    itself = columns // 2
-
     def target(offset):
-        there_col = lax.rem(col + itself + offset % columns, columns)
+        there_col = lax.rem(col + offset % columns, columns)
         there_row = lax.rem(row + offset // columns, rows)
         return there_col, there_row
 
     def origin(offset):
-        from_col = lax.rem(col + 2 * columns - itself - offset % columns, columns)
+        from_col = lax.rem(col + columns - offset % columns, columns)
         from_row = lax.rem(row + rows - offset // columns, rows)
         return from_col * rows + from_row
 
     def others(step):
-        lax.fori_loop(0, itself, step, 0)
-        lax.fori_loop(itself + 1, devices, step, 0)
+        lax.fori_loop(1, devices, step, 0)
 
     def greet(offset, carry):
         pl.semaphore_signal(barrier, inc=1, device_id=target(offset), device_id_type=MESH)
         return carry
 
     others(greet)
+    lax.fori_loop(0, slots * strips, start_load, 0)
+    phases = [
+        pltpu.make_async_copy(hbm, near, phase_sem.at[index])
+        for index, (hbm, near) in enumerate(((fine_hbm, fine_east), (coarse_hbm, coarse_east)))
+    ]
+    for copy in phases:
+        copy.start()
     cut[...] = jnp.broadcast_to(cut_row[...], (sz["local"], sz["local"])).T
     build_north_table(sz, fine_north, coarse_north, table_north)
 
@@ -442,6 +445,8 @@
         return carry
 
     lax.fori_loop(0, chunks, produce, 0)
+    for copy in phases:
+        copy.wait()
     build_east_table(sz, 0, fine_east, coarse_east, table_even)
     build_east_table(sz, 1, fine_east, coarse_east, table_odd)
 
@@ -547,7 +552,7 @@
             pltpu.VMEM((devices, share, local), f32),
             pltpu.VMEM((2, cells, cells), bf16),
         ),
-        in_specs=[anywhere] * 2 + [here] * 6,
+        in_specs=[anywhere] * 2 + [here] * 4 + [anywhere] * 2,
         out_specs=(here,) * 4,
         scratch_shapes=[
             pltpu.VMEM((slots, strips, 2, local, LANES), f32),
@@ -559,10 +564,13 @@
             pltpu.VMEM((chunks, sz["north"], local), f32),
             pltpu.VMEM((chunks - 1, devices, share, local), f32),
             pltpu.VMEM((2, lines, cells), bf16),
+            pltpu.VMEM(fine_east.shape, f32),
+            pltpu.VMEM(coarse_east.shape, f32),
             pltpu.SemaphoreType.DMA((2, slots, strips)),
             pltpu.SemaphoreType.DMA((chunks, devices)),
             pltpu.SemaphoreType.DMA((chunks, devices)),
             pltpu.SemaphoreType.DMA((chunks,)),
+            pltpu.SemaphoreType.DMA((2,)),
         ],
         compiler_params=pltpu.CompilerParams(
             collective_id=0, has_side_effects=True, vmem_limit_bytes=40 * 2**20

time: 205 us -> 204 us (level)
  no operation moved by 1% of the time
where the time goes in v3:
time: 204 us; the launch traced here: 203 us
  Pallas kernels  203 us (100%)
    pallas_call x1, Pallas kernels, on_device(): pl.pallas_call(functools.partial(exchange_kernel, sz), out_shape=(pltpu.V...  195 us
    pallas_call x1, Pallas kernels, on_device(): pl.pallas_call(functools.partial(finish_kernel, sz), out_shape=(out,) * 4...  7.24 us

profile of v3, /device:TPU:1, one launch (start us, length us, event | category | flops | bytes accessed | tf_op | source)
XLA Modules:
  0.0 203.4 jit_solution(4764601393744037206)
XLA Ops:
  0.6 0.0 copy-start
  0.6 195.5 %exchange.1 = (f32[3,512,2048]{2,1,0:T(8,128)S(1)}, f32[512,1024]{1,0:T(8,128)S(1)}, f32[32,64,128]{2,1,0:T(8,128)S(1)}, bf16[2,1024,1024]{2,1,0:T(8,128)(2,1)S(1)}) custom-call(f32[2,2,128,2048]{3,2,1,0:T(8,128)} %curl_hbm.1, f32[2,2,128,2048]{3,2,1,0:T(8,128)} %source_hbm.1, s32[1,128]{1,0:T(1,128)} %bitcast.1, f32[2,32,512]{2,1,0:T(8,128)} %constant.10.clone.fine_north, ...), custom_call_target="tpu_custom_call" | custom-call | tf_op jit(solution)/shard_map/exchange/pallas_call | solution.py:547
  196.1 0.0 copy-done
  196.2 7.2 %finish.1 = (f32[8,64,2048]{2,1,0:T(8,128)}, f32[8,64,2048]{2,1,0:T(8,128)}, f32[8,64,2048]{2,1,0:T(8,128)}, f32[8,64,2048]{2,1,0:T(8,128)}) custom-call(s32[8]{0:T(128)S(1)} %copy-done, f32[3,512,2048]{2,1,0:T(8,128)S(1)} %get-tuple-element.8.results, f32[512,1024]{1,0:T(8,128)S(1)} %get-tuple-element.9.even, f32[32,64,128]{2,1,0:T(8,128)S(1)} %get-tuple-element.10.last, ...), custom_call_target="tpu_custom_call" | custom-call | tf_op jit(solution)/shard_map/finish/pallas_call | solution.py:584
Async XLA Ops:
  0.6 195.5 %copy-start = (s32[8]{0:T(128)S(1)}, s32[8]{0:T(128)}, u32[]{:S(2)}) copy-start(s32[8]{0:T(128)} %level_slot.1) | copy-start | bytes 100
